TPU v7x, 128 devices: a whole 4x4x4 slice. The times are simulated.
128 devices in a mesh: rep: 2 (over y_lo), own: 64 (over x, z, y_hi, core).
Axes of the slice: x: 4, y: 4 (y_hi: 2, y_lo: 2; y = y_hi * 2 + y_lo), z: 4, core: 2. Of those that a mesh axis runs over, the one named last changes fastest.
Arguments:
- values: float32 [1048576, 128], P(('rep', 'own')), may hold values from -0.8 to 0.8
- key_ids: int32 [1048576], P(('rep', 'own')), may hold values from 0 to 262143, as said below
- heavy_ids: int32 [2048], replicated, may hold values from 0 to 262143, as said below
- block_offsets: int32 [128, 64], P(('rep', 'own')), may hold values from 0 to 8191, as said below
- block_counts: int32 [128, 64], P(('rep', 'own')), may hold values from 8 to 64, as said below
Outputs:
- light_sums: float32 [262144, 128], P('own')
- heavy_sums: float32 [2048, 128], P('own')
Inputs may be any that keep to these rules, and one draw needn't show every extreme that they name: `key_ids`: an event in block o of a device has a key in o * 4096 to (o + 1) * 4096 - 1 that is not a heavy key; every event outside all blocks has a heavy key. `heavy_ids`: distinct keys. `block_offsets`: on each device the blocks lie in the order of o, do not meet, and end by position 8192. `block_counts`: at most 64; one owner gets exactly 64 from every device.
All inputs are finite; a program needn't handle non-finite values.
Results may differ from a plain program's by a relative error of at most 0.000075.
Values sent between devices are 32-bit elements; how exact they have to be, the bound alone decides.
No kernel may reach another device: no remote copies, remote signals or barrier semaphores. Data moves between devices by JAX's collectives and lax.ppermute only.
A program may use at most 64 MiB of HBM per device.

v0:
```python
import math
import jax
import jax.numpy as jnp
from jax import lax
from jax.sharding import PartitionSpec as P

KEYS_DEV = 4096
CAP = 64


def over_pieces(x, axis):
    blocks = lax.all_gather(x, axis)
    return blocks.sum(axis=0)


def in_blocks(x, dim, size):
    lengths = x.shape
    blocks = x.reshape(*lengths[:dim], size, lengths[dim] // size, *lengths[dim + 1 :])
    return jnp.moveaxis(blocks, dim, 0)


def sum_at_owner(x, axis, dim):
    size = lax.axis_size(axis)
    blocks = lax.all_to_all(in_blocks(x, dim, size), axis, 0, 0, tiled=True)
    return jnp.sum(blocks, axis=0)


def key_sums(rows_in, row_keys, targets):
    slots = row_keys.shape[0]
    block_len = math.gcd(slots, 2048)
    count_blocks = slots // block_len
    rows_blocks = rows_in.reshape(count_blocks, block_len, rows_in.shape[1])
    keys_blocks = row_keys.reshape(count_blocks, block_len)

    def accumulate(running, pieces):
        rows_piece, keys_piece = pieces
        onehot = (targets[:, None] == keys_piece[None, :]).astype(jnp.float32)
        added = jnp.dot(
            onehot, rows_piece, precision=lax.Precision.HIGHEST, preferred_element_type=jnp.float32
        )
        return (running + added, None)

    start_sums = jnp.zeros((targets.shape[0], rows_in.shape[1]), jnp.float32)
    running, unused = lax.scan(accumulate, start_sums, (rows_blocks, keys_blocks))
    return running


def per_device(values, key_ids, heavy_ids, block_offsets, block_counts):
    owners = lax.axis_size("own")
    pairs = lax.axis_size("rep")
    own_index = lax.axis_index("own")
    rep_index = lax.axis_index("rep")
    width = values.shape[1]
    slot_cap = CAP
    padded_values = jnp.concatenate([values, jnp.zeros((slot_cap, width), jnp.float32)], axis=0)
    padded_keys = jnp.concatenate([key_ids, jnp.full((slot_cap,), -1, jnp.int32)], axis=0)
    slot_iota = jnp.arange(slot_cap, dtype=jnp.int32)
    positions = block_offsets[0][:, None] + slot_iota[None, :]
    valid = slot_iota[None, :] < block_counts[0][:, None]
    block_rows = jnp.where(valid[:, :, None], jnp.take(padded_values, positions, axis=0), 0.0)
    block_keys = jnp.where(valid, jnp.take(padded_keys, positions, axis=0), -1)
    half_keys = KEYS_DEV // 2
    owner_base = (jnp.arange(owners, dtype=jnp.int32) * KEYS_DEV)[:, None]
    which_half = jnp.where(block_keys >= 0, (block_keys - owner_base) // half_keys, -1)
    split_rows = jnp.stack(
        [jnp.where((which_half == side)[:, :, None], block_rows, 0.0) for side in range(pairs)],
        axis=0,
    )
    split_keys = jnp.stack(
        [jnp.where(which_half == side, block_keys, -1) for side in range(pairs)], axis=0
    )
    split_rows = split_rows.reshape(pairs * owners, slot_cap, width)
    split_keys = split_keys.reshape(pairs * owners, slot_cap)
    got_rows, got_keys = (
        lax.all_to_all(split_rows, ("rep", "own"), split_axis=0, concat_axis=0, tiled=True),
        lax.all_to_all(split_keys, ("rep", "own"), split_axis=0, concat_axis=0, tiled=True),
    )
    local_keys = jnp.where(
        got_keys >= 0, got_keys - own_index * KEYS_DEV - rep_index * half_keys, -1
    ).reshape(-1)
    owned_half = key_sums(
        got_rows.reshape(-1, width), local_keys, jnp.arange(half_keys, dtype=jnp.int32)
    )
    light_sums = lax.all_gather(owned_half, "rep", axis=0, tiled=True)
    partial_sums = key_sums(values, key_ids, heavy_ids)
    summed_pair = over_pieces(partial_sums, "rep")
    heavy_sums = sum_at_owner(summed_pair, "own", 0)
    return (light_sums, heavy_sums)


def solution(mesh):
    placed = (
        P(("rep", "own"), None),
        P(("rep", "own")),
        P(),
        P(("rep", "own"), None),
        P(("rep", "own"), None),
    )
    return jax.shard_map(
        per_device,
        mesh=mesh,
        in_specs=placed,
        out_specs=(P("own", None), P("own", None)),
        check_vma=False,
    )
```

profile of v0, /device:TPU:1, one launch (start us, length us, event | category | flops | bytes accessed | tf_op | source)
XLA Modules:
  0.0 223.6 jit_solution(12802448935710163705)
XLA Ops:
  7.2 0.7 compare_select_fusion.2
  7.9 0.1 reshape.542
  8.0 0.8 concatenate.6
  8.8 0.0 copy-start.3
  8.8 0.0 copy-start.4
  8.8 23.0 %gather_fusion = s32[4096]{0:T(1024)S(1)} fusion(s32[8256]{0:T(1024)S(1)} %concatenate.6, s32[4096]{0:T(1024)S(1)} %broadcast_clamp_fusion), kind=kCustom, calls=%fused_computation | custom fusion | bytes 49152 | tf_op jit(solution)/shard_map/jit(_take)/gather | solution.py:61
  31.8 0.1 gather.13
  31.9 0.0 copy-done.3
  31.9 0.0 copy-done.4
  31.9 0.1 compare_select_fusion.5
  32.0 0.6 pad_add_fusion
  32.6 11.5 %all-to-all-start = ((s32[128,1,64]{2,1,0:T(1,128)}), s32[128,1,64]{2,1,0:T(1,128)S(1)}, u32[]{:S(2)}, u32[]{:S(2)}) async-start(s32[128,1,64]{2,1,0:T(1,128)} %bitcast.2), calls=%async_computation | async-start | bytes 131072 | tf_op jit(solution)/shard_map/all_to_all | solution.py:76
  44.1 0.1 reshape.541
  44.2 0.1 broadcast_compare_fusion.1
  44.3 3.7 %concatenate.7 = f32[8256,128]{1,0:T(8,128)} pad(f32[8192,128]{1,0:T(8,128)} %param.9, f32[]{:T(128)} %constant.53.clone.1), padding=0_64x0_0 | pad | bytes 8421380 | tf_op jit(solution)/shard_map/concatenate | solution.py:55
  48.0 13.0 %gather_fusion.1 = f32[4096,128]{1,0:T(8,128)S(1)} fusion(f32[8256,128]{1,0:T(8,128)} %concatenate.7, s32[4096]{0:T(1024)S(1)} %broadcast_clamp_fusion), kind=kCustom, calls=%fused_computation.1 | custom fusion | bytes 4210688 | tf_op jit(solution)/shard_map/jit(_take)/gather | solution.py:60
  61.0 2.5 %fusion.19 = (f32[1,64,64,128]{3,2,1,0:T(8,128)S(1)}, f32[1,64,64,128]{3,2,1,0:T(8,128)S(1)}) fusion(f32[1,64,64,128]{3,2,1,0:T(8,128)S(1)} %bitcast.28, pred[64,64]{1,0:T(8,128)(4,1)S(1)} %get-tuple-element.118, pred[64,64]{1,0:T(8,128)(4,1)S(1)} %get-tuple-element.117, pred[64,64]{1,0:T(8,128)(4,1)S(1)} %get-tuple-element.111, ...), kind=kLoop, calls=%fused_computation.23 | loop fusion | flops 2097152 | bytes 6307840 | tf_op jit(solution)/shard_map/jit(_where)/select_n | solution.py:66
  63.5 2.3 %pad_maximum_fusion = f32[2,64,64,128]{3,2,1,0:T(8,128)} fusion(f32[1,64,64,128]{3,2,1,0:T(8,128)S(1)} %get-tuple-element.114, f32[1,64,64,128]{3,2,1,0:T(8,128)S(1)} %get-tuple-element.113), kind=kLoop, calls=%fused_computation.20 | loop fusion | flops 1048576 | bytes 8388608 | tf_op jit(solution)/shard_map/stack | solution.py:65
  65.8 0.0 all-to-all-done
  65.8 0.0 copy-start.2
  65.8 0.0 copy-start.5
  65.8 10.2 %all-to-all-start.1 = ((f32[128,64,128]{2,1,0:T(8,128)}), f32[128,64,128]{2,1,0:T(8,128)}, u32[]{:S(2)}, u32[]{:S(2)}) async-start(f32[128,64,128]{2,1,0:T(8,128)} %bitcast.27), calls=%async_computation.1 | async-start | bytes 8388608 | tf_op jit(solution)/shard_map/all_to_all | solution.py:75
  76.0 0.0 all-gather.6.cloned.1.call-start
  76.1 0.0 copy-done.2
  76.1 0.0 copy-done.5
  76.1 34.5 %while.23 = (s32[]{:T(128)}, f32[2048,128]{1,0:T(8,128)S(1)}, s32[2048]{0:T(1024)S(1)}, s32[4,2048]{1,0:T(4,128)S(1)}, f32[4,2048,128]{2,1,0:T(8,128)}, /*index=5*/s32[]{:T(128)}, s32[]{:T(128)}) while((s32[]{:T(128)}, f32[2048,128]{1,0:T(8,128)S(1)}, s32[2048]{0:T(1024)S(1)}, s32[4,2048]{1,0:T(4,128)S(1)}, ...), condition=%wide.region_3.4_spmd.clone, body=%wide.region_2.3_spmd.clone.sunk | while | flops 6447169536 | bytes 3179099 | solution.py:44
  76.1 8.6 %fusion.43 = f32[2048,128]{1,0:T(8,128)S(1)} fusion(s32[2048]{0:T(1024)S(1)} %bitcast.32, s32[2048]{0:T(1024)S(1)} %get-tuple-element.209, f32[2048,128]{1,0:T(8,128)S(1)} %get-tuple-element.201, f32[4,2048,128]{2,1,0:T(8,128)} %get-tuple-element.211, s32[]{:T(128)} %get-tuple-element.200, pred[]{:T(512)S(6)} %compare.33), kind=kOutput, calls=%fused_computation.15.clone.1 | convolution fusion | flops 6447169536 | bytes 3162625 | tf_op jit(solution)/shard_map/while/body/eval_jaxpr/dot_general | solution.py:38
  84.8 8.6 %fusion.43 = f32[2048,128]{1,0:T(8,128)S(1)} fusion(s32[2048]{0:T(1024)S(1)} %bitcast.32, s32[2048]{0:T(1024)S(1)} %get-tuple-element.209, f32[2048,128]{1,0:T(8,128)S(1)} %get-tuple-element.201, f32[4,2048,128]{2,1,0:T(8,128)} %get-tuple-element.211, s32[]{:T(128)} %get-tuple-element.200, pred[]{:T(512)S(6)} %compare.33), kind=kOutput, calls=%fused_computation.15.clone.1 | convolution fusion | flops 6447169536 | bytes 3162625 | tf_op jit(solution)/shard_map/while/body/eval_jaxpr/dot_general | solution.py:38
  93.4 8.6 %fusion.43 = f32[2048,128]{1,0:T(8,128)S(1)} fusion(s32[2048]{0:T(1024)S(1)} %bitcast.32, s32[2048]{0:T(1024)S(1)} %get-tuple-element.209, f32[2048,128]{1,0:T(8,128)S(1)} %get-tuple-element.201, f32[4,2048,128]{2,1,0:T(8,128)} %get-tuple-element.211, s32[]{:T(128)} %get-tuple-element.200, pred[]{:T(512)S(6)} %compare.33), kind=kOutput, calls=%fused_computation.15.clone.1 | convolution fusion | flops 6447169536 | bytes 3162625 | tf_op jit(solution)/shard_map/while/body/eval_jaxpr/dot_general | solution.py:38
  102.0 8.6 %fusion.43 = f32[2048,128]{1,0:T(8,128)S(1)} fusion(s32[2048]{0:T(1024)S(1)} %bitcast.32, s32[2048]{0:T(1024)S(1)} %get-tuple-element.209, f32[2048,128]{1,0:T(8,128)S(1)} %get-tuple-element.201, f32[4,2048,128]{2,1,0:T(8,128)} %get-tuple-element.211, s32[]{:T(128)} %get-tuple-element.200, pred[]{:T(512)S(6)} %compare.33), kind=kOutput, calls=%fused_computation.15.clone.1 | convolution fusion | flops 6447169536 | bytes 3162625 | tf_op jit(solution)/shard_map/while/body/eval_jaxpr/dot_general | solution.py:38
  110.6 0.0 copy-start.1
  110.6 1.0 copy-done.1
  111.6 0.0 all-gather.6.cloned.1.call-update
  111.6 0.2 all-gather.4.cloned.1.call-start
  111.9 0.2 fusion.20
  112.1 0.1 select_n.219
  112.2 17.3 %all-to-all-done.1 = f32[128,64,128]{2,1,0:T(8,128)} async-done(((f32[128,64,128]{2,1,0:T(8,128)}), f32[128,64,128]{2,1,0:T(8,128)}, u32[]{:S(2)}, u32[]{:S(2)}) %all-to-all-start.1) | async-done | bytes 4194336 | tf_op jit(solution)/shard_map/all_to_all | solution.py:75
  129.5 36.5 %while.22 = (s32[]{:T(128)}, f32[2048,128]{1,0:T(8,128)S(1)}, s32[4,2048]{1,0:T(4,128)S(1)}, f32[4,2048,128]{2,1,0:T(8,128)}, s32[]{:T(128)}, /*index=5*/s32[]{:T(128)}) while((s32[]{:T(128)}, f32[2048,128]{1,0:T(8,128)S(1)}, s32[4,2048]{1,0:T(4,128)S(1)}, f32[4,2048,128]{2,1,0:T(8,128)}, s32[]{:T(128)}, /*index=5*/s32[]{:T(128)}) %tuple.48), condition=%wide.region_1.2_spmd.clone, body=%wide.region_0.1_spmd.clone.sunk | while | flops 6447169536 | bytes 3170899 | solution.py:44
  129.5 9.1 %fusion.40 = f32[2048,128]{1,0:T(8,128)S(1)} fusion(s32[2048]{0:T(1024)S(1)} %bitcast.33, f32[2048,128]{1,0:T(8,128)S(1)} %get-tuple-element.182, f32[4,2048,128]{2,1,0:T(8,128)} %get-tuple-element.190, s32[]{:T(128)} %get-tuple-element.181, pred[]{:T(512)S(6)} %compare.32), kind=kOutput, calls=%fused_computation.6.clone.1 | convolution fusion | flops 6447169536 | bytes 3154433 | tf_op jit(solution)/shard_map/while/body/eval_jaxpr/dot_general | solution.py:38
  138.6 9.1 %fusion.40 = f32[2048,128]{1,0:T(8,128)S(1)} fusion(s32[2048]{0:T(1024)S(1)} %bitcast.33, f32[2048,128]{1,0:T(8,128)S(1)} %get-tuple-element.182, f32[4,2048,128]{2,1,0:T(8,128)} %get-tuple-element.190, s32[]{:T(128)} %get-tuple-element.181, pred[]{:T(512)S(6)} %compare.32), kind=kOutput, calls=%fused_computation.6.clone.1 | convolution fusion | flops 6447169536 | bytes 3154433 | tf_op jit(solution)/shard_map/while/body/eval_jaxpr/dot_general | solution.py:38
  147.8 9.1 %fusion.40 = f32[2048,128]{1,0:T(8,128)S(1)} fusion(s32[2048]{0:T(1024)S(1)} %bitcast.33, f32[2048,128]{1,0:T(8,128)S(1)} %get-tuple-element.182, f32[4,2048,128]{2,1,0:T(8,128)} %get-tuple-element.190, s32[]{:T(128)} %get-tuple-element.181, pred[]{:T(512)S(6)} %compare.32), kind=kOutput, calls=%fused_computation.6.clone.1 | convolution fusion | flops 6447169536 | bytes 3154433 | tf_op jit(solution)/shard_map/while/body/eval_jaxpr/dot_general | solution.py:38
  156.9 9.1 %fusion.40 = f32[2048,128]{1,0:T(8,128)S(1)} fusion(s32[2048]{0:T(1024)S(1)} %bitcast.33, f32[2048,128]{1,0:T(8,128)S(1)} %get-tuple-element.182, f32[4,2048,128]{2,1,0:T(8,128)} %get-tuple-element.190, s32[]{:T(128)} %get-tuple-element.181, pred[]{:T(512)S(6)} %compare.32), kind=kOutput, calls=%fused_computation.6.clone.1 | convolution fusion | flops 6447169536 | bytes 3154433 | tf_op jit(solution)/shard_map/while/body/eval_jaxpr/dot_general | solution.py:38
  166.0 0.0 copy-start
  166.0 1.0 copy-done
  167.0 0.0 all-gather.4.cloned.1.call-update
  167.0 0.0 all-gather.6.cloned.1.call-done
  167.0 1.8 reduce_sum.18
  168.9 30.6 %all_to_all.19 = f32[64,32,128]{2,1,0:T(8,128)S(1)} all-to-all(f32[64,32,128]{2,1,0:T(8,128)S(1)} %bitcast.30), channel_id=1, replica_groups=mesh['rep'=2,'own'=64] {'own'}, dimensions={0} | all-to-all | bytes 2097152 | tf_op jit(solution)/shard_map/all_to_all | solution.py:24
  199.4 0.7 reduce_sum.19
  200.1 13.6 %all-gather.4.cloned.1.call-done = f32[4096,128]{1,0:T(8,128)} async-done(((f32[2048,128]{1,0:T(8,128)}), f32[4096,128]{1,0:T(8,128)}) %all-gather.4.cloned.1.call-update) | async-done | bytes 2097168 | tf_op jit(solution)/shard_map/all_gather | solution.py:84
  213.8 3.0 %copy.20 = f32[4096,128]{1,0:T(8,128)} copy(f32[4096,128]{1,0:T(8,128)} %all-gather.4.cloned.1.call-done) | data formatting | bytes 4194304
  (14 shorter events, 0.1 us)
Async XLA Ops:
  8.8 23.1 %copy-start.3 = (s32[1,64]{1,0:T(1,128)S(1)}, s32[1,64]{1,0:T(1,128)}, u32[]{:S(2)}) copy-start(s32[1,64]{1,0:T(1,128)} %param.12) | copy-start | bytes 772
  8.8 23.1 %copy-start.4 = (s32[1,64]{1,0:T(1,128)S(1)}, s32[1,64]{1,0:T(1,128)}, u32[]{:S(2)}) copy-start(s32[1,64]{1,0:T(1,128)} %param.13) | copy-start | bytes 772
  32.6 33.1 %all-to-all-start = ((s32[128,1,64]{2,1,0:T(1,128)}), s32[128,1,64]{2,1,0:T(1,128)S(1)}, u32[]{:S(2)}, u32[]{:S(2)}) async-start(s32[128,1,64]{2,1,0:T(1,128)} %bitcast.2), calls=%async_computation | async-start | bytes 131072 | tf_op jit(solution)/shard_map/all_to_all | solution.py:76
  65.8 10.3 %copy-start.2 = (s32[8192]{0:T(1024)S(1)}, s32[8192]{0:T(1024)}, u32[]{:S(2)}) copy-start(s32[8192]{0:T(1024)} %param.10) | copy-start | bytes 98308
  65.8 10.3 %copy-start.5 = (s32[2048]{0:T(1024)S(1)}, s32[2048]{0:T(1024)}, u32[]{:S(2)}) copy-start(s32[2048]{0:T(1024)} %param.11) | copy-start | bytes 24580
  65.8 63.7 %all-to-all-start.1 = ((f32[128,64,128]{2,1,0:T(8,128)}), f32[128,64,128]{2,1,0:T(8,128)}, u32[]{:S(2)}, u32[]{:S(2)}) async-start(f32[128,64,128]{2,1,0:T(8,128)} %bitcast.27), calls=%async_computation.1 | async-start | bytes 8388608 | tf_op jit(solution)/shard_map/all_to_all | solution.py:75
  76.0 91.0 %all-gather.6.cloned.1.call-start = ((), (), s32[]{:S(2)}) async-start(), calls=%async_computation.4 | async-start | bytes 3145728 | tf_op jit(solution)/shard_map/all_gather | solution.py:12
  110.6 1.0 copy-start.1
  111.6 102.2 %all-gather.4.cloned.1.call-start = ((), (), s32[]{:S(2)}) async-start(), calls=%async_computation.3 | async-start | bytes 3145728 | tf_op jit(solution)/shard_map/all_gather | solution.py:84
  166.0 1.0 copy-start
Sparse Core Ops, SparseCore 0:
  111.7 36.9 all-gather.5
  167.1 46.5 all-gather.3
where the time goes:
time: 224 us
  matrix products  70.7 us (32%)
  local copies, waits for them, and re-layouts  45.9 us (20%)
  waiting for transfers between devices  31 us (14%)
  blocking collectives  30.6 us (14%)
  starting transfers between devices  22 us (10%)
  between operations  14.2 us (6%)
  other arithmetic  9.15 us (4%)
    dot_general x8, matrix products, accumulate(): jnp.dot(onehot, rows_piece, precision=lax.Precision.HIGHEST, preferred_el...  70.7 us
    all_to_all x1, blocking collectives, sum_at_owner(): blocks = lax.all_to_all(in_blocks(x, dim, size), axis, 0, 0, tiled=True)  30.6 us
    gather x3, local copies, waits for them, and re-layouts, per_device(): block_keys = jnp.where(valid, jnp.take(padded_keys, positions, axis=0), -1)  23.2 us
    all_to_all x1, waiting for transfers between devices, per_device(): lax.all_to_all(split_rows, ('rep', 'own'), split_axis=0, concat_axis=0, t...  17.3 us
    all_gather x1, waiting for transfers between devices, per_device(): light_sums = lax.all_gather(owned_half, 'rep', axis=0, tiled=True)  13.6 us
    gather x1, local copies, waits for them, and re-layouts, per_device(): jnp.take(padded_values, positions, axis=0)  13 us
    all_to_all x1, starting transfers between devices, per_device(): lax.all_to_all(split_keys, ('rep', 'own'), split_axis=0, concat_axis=0, t...  11.5 us
    all_to_all x1, starting transfers between devices, per_device(): lax.all_to_all(split_rows, ('rep', 'own'), split_axis=0, concat_axis=0, t...  10.2 us
  transfers between devices with their start and end apart: 4, of which 2 were waited for; matrix products, arithmetic and copies ran while one was open for 43% of the time, Pallas kernels for 0%

commit v1 on v0

--- a/solution.py
+++ b/solution.py
@@ -81,7 +81,13 @@
     owned_half = key_sums(
         got_rows.reshape(-1, width), local_keys, jnp.arange(half_keys, dtype=jnp.int32)
     )
-    light_sums = lax.all_gather(owned_half, "rep", axis=0, tiled=True)
+
+    def place_ratios(dim_i, content):
+        opened = jnp.stack([content for _ in range(lax.axis_size("rep"))], 0)
+        piece_now = lax.all_to_all(opened, axis_name="rep", split_axis=0, concat_axis=0)
+        return jnp.concatenate(piece_now, dim_i)
+
+    light_sums = place_ratios(0, owned_half)
     partial_sums = key_sums(values, key_ids, heavy_ids)
     summed_pair = over_pieces(partial_sums, "rep")
     heavy_sums = sum_at_owner(summed_pair, "own", 0)

time: 224 us -> 238 us (1.062)
  blocking collectives: 30.6 us -> 0 us
  waiting for transfers between devices: 31 us -> 60.5 us
  starting transfers between devices: 22 us -> 36.5 us
  local copies, waits for them, and re-layouts: 45.9 us -> 43.2 us
  other arithmetic: 9.15 us -> 11.6 us
    all_gather x1, waiting for transfers between devices: 0.02 us -> 36.7 us  [over_pieces(): blocks = lax.all_gather(x, axis)]
    all_to_all x1 -> x0, blocking collectives: 30.6 us -> none  [sum_at_owner(): blocks = lax.all_to_all(in_blocks(x, dim, size), axis, 0, 0, tiled=True)]
    all_to_all x0 -> x2, waiting for transfers between devices: none -> 23.7 us  [the longest x1 23.7 us: place_ratios(): lax.all_to_all(opened, axis_name='rep', split_axis=0, concat_axis=0)]
    all_to_all x1, waiting for transfers between devices: 17.3 us -> 0.01 us  [per_device(): lax.all_to_all(split_rows, ('rep', 'own'), split_axis=0, concat_axis=0, t...]
    all_to_all x0 -> x2, starting transfers between devices: none -> 14.7 us  [the longest x1 10.9 us: sum_at_owner(): blocks = lax.all_to_all(in_blocks(x, dim, size), axis, 0, 0, tiled=True)]
    all_gather x1 -> x0, waiting for transfers between devices: 13.6 us -> none  [per_device(): light_sums = lax.all_gather(owned_half, 'rep', axis=0, tiled=True)]
    unnamed x13 -> x11, local copies, waits for them, and re-layouts: 5.01 us -> 2.3 us
  transfers between devices with their start and end apart: 4 -> 5, of which waited for: 2 -> 2; matrix products, arithmetic and copies ran while one was open for 43% -> 41% of each run, Pallas kernels for 0% -> 0%
where the time goes in v1:
time: 238 us; the launch traced here: 237 us
  matrix products  70.7 us (30%)
  waiting for transfers between devices  60.5 us (25%)
  local copies, waits for them, and re-layouts  43.2 us (18%)
  starting transfers between devices  36.5 us (15%)
  between operations  14.2 us (6%)
  other arithmetic  11.6 us (5%)
    dot_general x8, matrix products, accumulate(): jnp.dot(onehot, rows_piece, precision=lax.Precision.HIGHEST, preferred_el...  70.7 us
    all_gather x1, waiting for transfers between devices, over_pieces(): blocks = lax.all_gather(x, axis)  36.7 us
    all_to_all x1, waiting for transfers between devices, place_ratios(): lax.all_to_all(opened, axis_name='rep', split_axis=0, concat_axis=0)  23.7 us
    gather x3, local copies, waits for them, and re-layouts, per_device(): block_keys = jnp.where(valid, jnp.take(padded_keys, positions, axis=0), -1)  23.2 us
    gather x1, local copies, waits for them, and re-layouts, per_device(): jnp.take(padded_values, positions, axis=0)  13 us
    all_to_all x1, starting transfers between devices, per_device(): lax.all_to_all(split_keys, ('rep', 'own'), split_axis=0, concat_axis=0, t...  11.5 us
    all_to_all x1, starting transfers between devices, sum_at_owner(): blocks = lax.all_to_all(in_blocks(x, dim, size), axis, 0, 0, tiled=True)  10.9 us
    all_to_all x1, starting transfers between devices, per_device(): lax.all_to_all(split_rows, ('rep', 'own'), split_axis=0, concat_axis=0, t...  10.2 us
  transfers between devices with their start and end apart: 5, of which 2 were waited for; matrix products, arithmetic and copies ran while one was open for 41% of the time, Pallas kernels for 0%

profile of v1, /device:TPU:1, one launch (start us, length us, event | category | flops | bytes accessed | tf_op | source)
XLA Modules:
  0.0 236.9 jit_solution(17682818753660597475)
XLA Ops:
  7.2 0.7 compare_select_fusion.2
  7.9 0.1 reshape.546
  8.0 0.8 concatenate.6
  8.8 0.0 copy-start.2
  8.8 0.0 copy-start.3
  8.8 23.0 %gather_fusion = s32[4096]{0:T(1024)S(1)} fusion(s32[8256]{0:T(1024)S(1)} %concatenate.6, s32[4096]{0:T(1024)S(1)} %broadcast_clamp_fusion), kind=kCustom, calls=%fused_computation | custom fusion | bytes 49152 | tf_op jit(solution)/shard_map/jit(_take)/gather | solution.py:61
  31.8 0.1 gather.13
  31.9 0.0 copy-done.2
  31.9 0.0 copy-done.3
  31.9 0.1 compare_select_fusion.5
  32.0 0.6 pad_add_fusion
  32.6 11.5 %all-to-all-start = ((s32[128,1,64]{2,1,0:T(1,128)}), s32[128,1,64]{2,1,0:T(1,128)S(1)}, u32[]{:S(2)}, u32[]{:S(2)}) async-start(s32[128,1,64]{2,1,0:T(1,128)} %bitcast.2), calls=%async_computation | async-start | bytes 131072 | tf_op jit(solution)/shard_map/all_to_all | solution.py:76
  44.1 0.1 reshape.545
  44.2 0.1 broadcast_compare_fusion.1
  44.3 3.7 %concatenate.7 = f32[8256,128]{1,0:T(8,128)} pad(f32[8192,128]{1,0:T(8,128)} %param.9, f32[]{:T(128)} %constant.53.clone.1), padding=0_64x0_0 | pad | bytes 8421380 | tf_op jit(solution)/shard_map/concatenate | solution.py:55
  48.0 13.0 %gather_fusion.1 = f32[4096,128]{1,0:T(8,128)S(1)} fusion(f32[8256,128]{1,0:T(8,128)} %concatenate.7, s32[4096]{0:T(1024)S(1)} %broadcast_clamp_fusion), kind=kCustom, calls=%fused_computation.1 | custom fusion | bytes 4210688 | tf_op jit(solution)/shard_map/jit(_take)/gather | solution.py:60
  61.0 2.5 %fusion.19 = (f32[1,64,64,128]{3,2,1,0:T(8,128)S(1)}, f32[1,64,64,128]{3,2,1,0:T(8,128)S(1)}) fusion(f32[1,64,64,128]{3,2,1,0:T(8,128)S(1)} %bitcast.30, pred[64,64]{1,0:T(8,128)(4,1)S(1)} %get-tuple-element.118, pred[64,64]{1,0:T(8,128)(4,1)S(1)} %get-tuple-element.117, pred[64,64]{1,0:T(8,128)(4,1)S(1)} %get-tuple-element.111, ...), kind=kLoop, calls=%fused_computation.24 | loop fusion | flops 2097152 | bytes 6307840 | tf_op jit(solution)/shard_map/jit(_where)/select_n | solution.py:66
  63.5 0.0 copy-start.1
  63.5 2.3 pad_maximum_fusion
  65.8 0.0 copy-done.1
  65.8 0.0 all-to-all-done
  65.8 0.0 copy-start.4
  65.8 10.2 %all-to-all-start.1 = ((f32[128,64,128]{2,1,0:T(8,128)}), f32[128,64,128]{2,1,0:T(8,128)}, u32[]{:S(2)}, u32[]{:S(2)}) async-start(f32[128,64,128]{2,1,0:T(8,128)} %bitcast.29), calls=%async_computation.1 | async-start | bytes 8388608 | tf_op jit(solution)/shard_map/all_to_all | solution.py:75
  76.1 0.0 all-gather.3.cloned.1.call-start
  76.1 0.0 copy-done.4
  76.1 34.5 %while.23 = (s32[]{:T(128)}, f32[2048,128]{1,0:T(8,128)S(1)}, s32[2048]{0:T(1024)S(1)}, s32[4,2048]{1,0:T(4,128)S(1)}, f32[4,2048,128]{2,1,0:T(8,128)}, /*index=5*/s32[]{:T(128)}, s32[]{:T(128)}) while((s32[]{:T(128)}, f32[2048,128]{1,0:T(8,128)S(1)}, s32[2048]{0:T(1024)S(1)}, s32[4,2048]{1,0:T(4,128)S(1)}, ...), condition=%wide.region_3.4_spmd.clone, body=%wide.region_2.3_spmd.clone.sunk | while | flops 6447169536 | bytes 3179099 | solution.py:44
  76.2 8.6 %fusion.43 = f32[2048,128]{1,0:T(8,128)S(1)} fusion(s32[2048]{0:T(1024)S(1)} %bitcast.35, s32[2048]{0:T(1024)S(1)} %get-tuple-element.209, f32[2048,128]{1,0:T(8,128)S(1)} %get-tuple-element.201, f32[4,2048,128]{2,1,0:T(8,128)} %get-tuple-element.211, s32[]{:T(128)} %get-tuple-element.200, pred[]{:T(512)S(6)} %compare.33), kind=kOutput, calls=%fused_computation.15.clone.1 | convolution fusion | flops 6447169536 | bytes 3162625 | tf_op jit(solution)/shard_map/while/body/eval_jaxpr/dot_general | solution.py:38
  84.8 8.6 %fusion.43 = f32[2048,128]{1,0:T(8,128)S(1)} fusion(s32[2048]{0:T(1024)S(1)} %bitcast.35, s32[2048]{0:T(1024)S(1)} %get-tuple-element.209, f32[2048,128]{1,0:T(8,128)S(1)} %get-tuple-element.201, f32[4,2048,128]{2,1,0:T(8,128)} %get-tuple-element.211, s32[]{:T(128)} %get-tuple-element.200, pred[]{:T(512)S(6)} %compare.33), kind=kOutput, calls=%fused_computation.15.clone.1 | convolution fusion | flops 6447169536 | bytes 3162625 | tf_op jit(solution)/shard_map/while/body/eval_jaxpr/dot_general | solution.py:38
  93.4 8.6 %fusion.43 = f32[2048,128]{1,0:T(8,128)S(1)} fusion(s32[2048]{0:T(1024)S(1)} %bitcast.35, s32[2048]{0:T(1024)S(1)} %get-tuple-element.209, f32[2048,128]{1,0:T(8,128)S(1)} %get-tuple-element.201, f32[4,2048,128]{2,1,0:T(8,128)} %get-tuple-element.211, s32[]{:T(128)} %get-tuple-element.200, pred[]{:T(512)S(6)} %compare.33), kind=kOutput, calls=%fused_computation.15.clone.1 | convolution fusion | flops 6447169536 | bytes 3162625 | tf_op jit(solution)/shard_map/while/body/eval_jaxpr/dot_general | solution.py:38
  102.0 8.6 %fusion.43 = f32[2048,128]{1,0:T(8,128)S(1)} fusion(s32[2048]{0:T(1024)S(1)} %bitcast.35, s32[2048]{0:T(1024)S(1)} %get-tuple-element.209, f32[2048,128]{1,0:T(8,128)S(1)} %get-tuple-element.201, f32[4,2048,128]{2,1,0:T(8,128)} %get-tuple-element.211, s32[]{:T(128)} %get-tuple-element.200, pred[]{:T(512)S(6)} %compare.33), kind=kOutput, calls=%fused_computation.15.clone.1 | convolution fusion | flops 6447169536 | bytes 3162625 | tf_op jit(solution)/shard_map/while/body/eval_jaxpr/dot_general | solution.py:38
  110.6 0.0 copy-start
  110.6 1.0 copy-done
  111.6 0.0 all-gather.3.cloned.1.call-update
  111.6 0.2 fusion.20
  111.9 0.1 select_n.219
  111.9 36.7 %all-gather.3.cloned.1.call-done = f32[4096,128]{1,0:T(8,128)} async-done(((f32[2048,128]{1,0:T(8,128)}), f32[4096,128]{1,0:T(8,128)}) %all-gather.3.cloned.1.call-update) | async-done | bytes 2097168 | tf_op jit(solution)/shard_map/all_gather | solution.py:12
  148.7 2.8 %reduce_sum.18 = f32[2048,128]{1,0:T(8,128)} reduce(f32[2,2048,128]{2,1,0:T(8,128)} %bitcast.33, f32[]{:T(128)} %constant.53.clone.1), dimensions={0}, to_apply=%region_4.5 | reduce | flops 262144 | bytes 3145732 | tf_op jit(solution)/shard_map/reduce_sum | solution.py:13
  151.5 0.0 all-to-all-done.1
  151.5 10.9 %all-to-all-start.3 = ((f32[64,32,128]{2,1,0:T(8,128)}), f32[64,32,128]{2,1,0:T(8,128)S(1)}, u32[]{:S(2)}, u32[]{:S(2)}) async-start(f32[64,32,128]{2,1,0:T(8,128)} %bitcast.10), calls=%async_computation.3 | async-start | bytes 2097152 | tf_op jit(solution)/shard_map/all_to_all | solution.py:24
  162.5 36.6 %while.22 = (s32[]{:T(128)}, f32[2048,128]{1,0:T(8,128)S(1)}, s32[4,2048]{1,0:T(4,128)S(1)}, f32[4,2048,128]{2,1,0:T(8,128)}, s32[]{:T(128)}, /*index=5*/s32[]{:T(128)}) while((s32[]{:T(128)}, f32[2048,128]{1,0:T(8,128)S(1)}, s32[4,2048]{1,0:T(4,128)S(1)}, f32[4,2048,128]{2,1,0:T(8,128)}, s32[]{:T(128)}, /*index=5*/s32[]{:T(128)}) %tuple.48), condition=%wide.region_1.2_spmd.clone, body=%wide.region_0.1_spmd.clone.sunk | while | flops 6447169536 | bytes 3170899 | solution.py:44
  162.5 9.1 %fusion.40 = f32[2048,128]{1,0:T(8,128)S(1)} fusion(s32[2048]{0:T(1024)S(1)} %bitcast.36, f32[2048,128]{1,0:T(8,128)S(1)} %get-tuple-element.182, f32[4,2048,128]{2,1,0:T(8,128)} %get-tuple-element.190, s32[]{:T(128)} %get-tuple-element.181, pred[]{:T(512)S(6)} %compare.32), kind=kOutput, calls=%fused_computation.6.clone.1 | convolution fusion | flops 6447169536 | bytes 3154433 | tf_op jit(solution)/shard_map/while/body/eval_jaxpr/dot_general | solution.py:38
  171.6 9.1 %fusion.40 = f32[2048,128]{1,0:T(8,128)S(1)} fusion(s32[2048]{0:T(1024)S(1)} %bitcast.36, f32[2048,128]{1,0:T(8,128)S(1)} %get-tuple-element.182, f32[4,2048,128]{2,1,0:T(8,128)} %get-tuple-element.190, s32[]{:T(128)} %get-tuple-element.181, pred[]{:T(512)S(6)} %compare.32), kind=kOutput, calls=%fused_computation.6.clone.1 | convolution fusion | flops 6447169536 | bytes 3154433 | tf_op jit(solution)/shard_map/while/body/eval_jaxpr/dot_general | solution.py:38
  180.8 9.1 %fusion.40 = f32[2048,128]{1,0:T(8,128)S(1)} fusion(s32[2048]{0:T(1024)S(1)} %bitcast.36, f32[2048,128]{1,0:T(8,128)S(1)} %get-tuple-element.182, f32[4,2048,128]{2,1,0:T(8,128)} %get-tuple-element.190, s32[]{:T(128)} %get-tuple-element.181, pred[]{:T(512)S(6)} %compare.32), kind=kOutput, calls=%fused_computation.6.clone.1 | convolution fusion | flops 6447169536 | bytes 3154433 | tf_op jit(solution)/shard_map/while/body/eval_jaxpr/dot_general | solution.py:38
  189.9 9.1 %fusion.40 = f32[2048,128]{1,0:T(8,128)S(1)} fusion(s32[2048]{0:T(1024)S(1)} %bitcast.36, f32[2048,128]{1,0:T(8,128)S(1)} %get-tuple-element.182, f32[4,2048,128]{2,1,0:T(8,128)} %get-tuple-element.190, s32[]{:T(128)} %get-tuple-element.181, pred[]{:T(512)S(6)} %compare.32), kind=kOutput, calls=%fused_computation.6.clone.1 | convolution fusion | flops 6447169536 | bytes 3154433 | tf_op jit(solution)/shard_map/while/body/eval_jaxpr/dot_general | solution.py:38
  199.0 1.5 pad_maximum_fusion.1
  200.5 0.0 all-to-all-done.3
  200.5 3.8 %all-to-all-start.2 = ((f32[2,2048,128]{2,1,0:T(8,128)}), f32[2,2048,128]{2,1,0:T(8,128)S(1)}, u32[]{:S(2)}, u32[]{:S(2)}) async-start(f32[2,2048,128]{2,1,0:T(8,128)} %pad_maximum_fusion.1), calls=%async_computation.2 | async-start | bytes 4194304 | tf_op jit(solution)/shard_map/all_to_all | solution.py:87
  204.3 0.7 reduce_sum.19
  205.0 23.7 %all-to-all-done.2 = f32[2,2048,128]{2,1,0:T(8,128)S(1)} async-done(((f32[2,2048,128]{2,1,0:T(8,128)}), f32[2,2048,128]{2,1,0:T(8,128)S(1)}, u32[]{:S(2)}, u32[]{:S(2)}) %all-to-all-start.2) | async-done | bytes 2097184 | tf_op jit(solution)/shard_map/all_to_all | solution.py:87
  228.7 1.3 copy.20
  (14 shorter events, 0.1 us)
Async XLA Ops:
  8.8 23.1 %copy-start.2 = (s32[1,64]{1,0:T(1,128)S(1)}, s32[1,64]{1,0:T(1,128)}, u32[]{:S(2)}) copy-start(s32[1,64]{1,0:T(1,128)} %param.12) | copy-start | bytes 772
  8.8 23.1 %copy-start.3 = (s32[1,64]{1,0:T(1,128)S(1)}, s32[1,64]{1,0:T(1,128)}, u32[]{:S(2)}) copy-start(s32[1,64]{1,0:T(1,128)} %param.13) | copy-start | bytes 772
  32.6 33.2 %all-to-all-start = ((s32[128,1,64]{2,1,0:T(1,128)}), s32[128,1,64]{2,1,0:T(1,128)S(1)}, u32[]{:S(2)}, u32[]{:S(2)}) async-start(s32[128,1,64]{2,1,0:T(1,128)} %bitcast.2), calls=%async_computation | async-start | bytes 131072 | tf_op jit(solution)/shard_map/all_to_all | solution.py:76
  63.5 2.3 copy-start.1
  65.8 10.3 %copy-start.4 = (s32[2048]{0:T(1024)S(1)}, s32[2048]{0:T(1024)}, u32[]{:S(2)}) copy-start(s32[2048]{0:T(1024)} %param.11) | copy-start | bytes 24580
  65.8 85.7 %all-to-all-start.1 = ((f32[128,64,128]{2,1,0:T(8,128)}), f32[128,64,128]{2,1,0:T(8,128)}, u32[]{:S(2)}, u32[]{:S(2)}) async-start(f32[128,64,128]{2,1,0:T(8,128)} %bitcast.29), calls=%async_computation.1 | async-start | bytes 8388608 | tf_op jit(solution)/shard_map/all_to_all | solution.py:75
  76.1 72.6 %all-gather.3.cloned.1.call-start = ((), (), s32[]{:S(2)}) async-start(), calls=%async_computation.4 | async-start | bytes 3145728 | tf_op jit(solution)/shard_map/all_gather | solution.py:12
  110.6 1.0 copy-start
  151.5 49.0 %all-to-all-start.3 = ((f32[64,32,128]{2,1,0:T(8,128)}), f32[64,32,128]{2,1,0:T(8,128)S(1)}, u32[]{:S(2)}, u32[]{:S(2)}) async-start(f32[64,32,128]{2,1,0:T(8,128)} %bitcast.10), calls=%async_computation.3 | async-start | bytes 2097152 | tf_op jit(solution)/shard_map/all_to_all | solution.py:24
  200.5 28.2 %all-to-all-start.2 = ((f32[2,2048,128]{2,1,0:T(8,128)}), f32[2,2048,128]{2,1,0:T(8,128)S(1)}, u32[]{:S(2)}, u32[]{:S(2)}) async-start(f32[2,2048,128]{2,1,0:T(8,128)} %pad_maximum_fusion.1), calls=%async_computation.2 | async-start | bytes 4194304 | tf_op jit(solution)/shard_map/all_to_all | solution.py:87
Sparse Core Ops, SparseCore 0:
  111.7 36.9 all-gather.2
